TPU v7x, 32 devices: a whole 2x2x4 slice. The times are simulated.
32 devices in a mesh: rows: 16 (over z, y, x), cols: 2 (over core).
Axes of the slice: x: 2, y: 2, z: 4, core: 2. Of those that a mesh axis runs over, the one named last changes fastest.
Arguments:
- design: float32 [16384, 512], P('rows', 'cols'), may hold values from -24 to 24
- signs: int32 [16384], P('rows'), may hold values from -1 to 1, as said below
- kept: int32 [1024], replicated, may hold values from 0 to 16383, as said below
Outputs:
- sketch: float32 [1024, 512], P('rows', 'cols')
- factor: float32 [512, 512], P(None, 'cols')
Inputs may be any that keep to these rules, and one draw needn't show every extreme that they name: `signs`: each entry is +1 or -1. `kept`: distinct and increasing.
All inputs are finite; a program needn't handle non-finite values.
Results may differ from a plain program's by a relative error of at most 0.0003.
Values sent between devices are 32-bit elements; how exact they have to be, the bound alone decides.
A program may use at most 64 MiB of HBM per device.

v0:
```python
import math
import jax
import jax.numpy as jnp
from jax import lax
from jax.sharding import PartitionSpec as P


def hadamard(order):
    matrix = jnp.ones((1, 1), jnp.float32)
    base = jnp.array([[1.0, 1.0], [1.0, -1.0]], jnp.float32)
    while matrix.shape[0] < order:
        matrix = jnp.kron(matrix, base)
    return matrix


def bit_parity(value):
    folded = value
    for amount in (16, 8, 4, 2, 1):
        folded = jnp.bitwise_xor(folded, jnp.right_shift(folded, amount))
    return jnp.bitwise_and(folded, 1)


def local_transform(flipped):
    length, width = flipped.shape
    outer = length // 128
    inner_table = hadamard(128)
    outer_table = hadamard(outer)
    blocks = flipped.reshape(outer, 128, width)
    mixed = jnp.einsum("pb,abc->apc", inner_table, blocks, precision=lax.Precision.HIGHEST)
    mixed = jnp.einsum("qa,apc->qpc", outer_table, mixed, precision=lax.Precision.HIGHEST)
    return mixed.reshape(length, width)


def signed_rows(transformed, kept_part, device_row, total_rows):
    length = transformed.shape[0]
    kept_blocks = kept_part // length
    offsets = kept_part - kept_blocks * length
    parity = bit_parity(jnp.bitwise_and(kept_blocks, device_row))
    factor = (1.0 - 2.0 * parity.astype(jnp.float32)) / math.sqrt(total_rows)
    return jnp.take(transformed, offsets, axis=0) * factor[:, None]


def source_total(received):
    return jnp.sum(received, axis=0)


def body(design, signs, kept):
    flipped = design * signs.astype(jnp.float32)[:, None]
    transformed = local_transform(flipped)
    device_row = lax.axis_index("rows")
    groups = lax.axis_size("rows")
    length = transformed.shape[0]
    widths = transformed.shape[1]
    total_rows = length * groups
    per_device = kept.shape[0] // groups
    outgoing = signed_rows(transformed, kept, device_row, total_rows)
    outgoing = outgoing.reshape(groups, per_device, widths)
    sketch = source_total(lax.all_to_all(outgoing, "rows", split_axis=0, concat_axis=0, tiled=True))
    column = lax.axis_index("cols")
    whole = lax.all_gather(sketch, "cols", axis=1, tiled=True)
    kept_total = kept.shape[0]
    partial_gram = jnp.dot(
        whole.T, whole, precision=lax.Precision.HIGHEST, preferred_element_type=jnp.float32
    )
    gram = lax.psum(partial_gram, "rows") / kept_total
    factor = jnp.linalg.cholesky(gram).T
    return (sketch, lax.dynamic_slice_in_dim(factor, column * widths, widths, 1))


def solution(mesh):
    placed = (P("rows", "cols"), P("rows"), P())
    return jax.shard_map(
        body,
        mesh=mesh,
        in_specs=placed,
        out_specs=(P("rows", "cols"), P(None, "cols")),
        check_vma=False,
    )
```

profile of v0, /device:TPU:0, one launch (start us, length us, event | category | flops | bytes accessed | tf_op | source)
XLA Modules:
  0.0 271.5 jit_solution(705625595434788475)
XLA Ops:
  7.2 0.8 broadcast_multiply_fusion.7
  8.1 0.8 broadcast_multiply_fusion.6
  9.0 0.7 broadcast_clamp_fusion
  9.7 0.7 compare_and_fusion
  10.4 0.8 broadcast_multiply_fusion.5
  11.3 0.8 broadcast_multiply_fusion.4
  12.2 0.9 broadcast_multiply_fusion.2
  13.1 0.6 mul.278
  13.8 3.1 %broadcast_multiply_fusion = f32[64,2,64,2]{3,2,1,0:T(8,128)} fusion(f32[2,2]{1,0:T(2,128)} %constant.202.clone, f32[64,64]{1,0:T(8,128)S(1)} %mul.278), kind=kLoop, calls=%fused_computation.1 | loop fusion | flops 16384 | bytes 81936 | tf_op jit(solution)/shard_map/jit(kron)/mul | solution.py:12
  16.9 4.0 %reshape.202 = f32[128,128,1]{1,0,2:T(8,128)S(1)} reshape(f32[64,2,64,2]{3,2,1,0:T(8,128)} %broadcast_multiply_fusion) | data formatting | bytes 131072 | tf_op jit(solution)/shard_map/jit(kron)/mul | solution.py:12
  21.1 1.8 fusion.23
  22.9 0.5 copy.14
  23.4 1.0 fusion.1
  25.0 3.5 %gather_fusion = f32[1024,256]{1,0:T(8,128)S(1)} fusion(f32[1024,256]{1,0:T(8,128)S(1)} %bitcast.43, s32[1024]{0:T(1024)S(1)} %broadcast_clamp_fusion), kind=kCustom, calls=%fused_computation | custom fusion | bytes 2101248 | tf_op jit(solution)/shard_map/jit(_take)/gather | solution.py:40
  28.8 34.5 %all_to_all.5 = f32[16,64,256]{2,1,0:T(8,128)S(1)} all-to-all(f32[16,64,256]{2,1,0:T(8,128)S(1)} %select_multiply_fusion), channel_id=1, replica_groups=mesh['rows'=16,'cols'=2] {'rows'}, dimensions={0} | all-to-all | bytes 2097152 | tf_op jit(solution)/shard_map/all_to_all | solution.py:58
  63.3 2.1 all_gather.3
  65.4 2.1 fusion.24
  67.5 110.9 %all-reduce.3.cloned.1.call-done = f32[512,512]{0,1:T(8,128)} async-done(((f32[512,512]{0,1:T(8,128)}), f32[512,512]{0,1:T(8,128)}) %all-reduce.3.cloned.1.call-update) | async-done | bytes 1048592 | tf_op jit(solution)/shard_map/psum | solution.py:65
  178.4 1.4 broadcast_multiply_fusion.1
  180.4 11.7 %cholesky.104 = f32[128,128]{1,0:T(8,128)S(1)} custom-call(f32[128,128]{1,0:T(8,128)S(1)} %cholesky.266), custom_call_target="Cholesky" | custom-call | tf_op jit(solution)/shard_map/jit(cholesky)/cholesky | solution.py:66
  192.3 9.8 %custom-call.27 = f32[1,128,128]{1,2,0:T(8,128)S(1)} custom-call(f32[1,128,128]{2,1,0:T(8,128)S(1)} %get-tuple-element.15), custom_call_target="InvertDiagBlocksLowerTriangular" | custom-call | tf_op jit(solution)/shard_map/jit(cholesky)/cholesky | solution.py:66
  202.7 11.7 %cholesky.217 = f32[128,128]{1,0:T(8,128)S(1)} custom-call(f32[128,128]{1,0:T(8,128)S(1)} %cholesky.270), custom_call_target="Cholesky" | custom-call | tf_op jit(solution)/shard_map/jit(cholesky)/cholesky | solution.py:66
  214.5 9.9 %custom-call.28 = f32[1,128,128]{1,2,0:T(8,128)S(1)} custom-call(f32[1,128,128]{2,1,0:T(8,128)S(1)} %get-tuple-element.12), custom_call_target="InvertDiagBlocksLowerTriangular" | custom-call | tf_op jit(solution)/shard_map/jit(cholesky)/cholesky | solution.py:66
  224.7 0.4 convolution_subtract_fusion.1
  225.1 11.7 %cholesky.238 = f32[128,128]{1,0:T(8,128)S(1)} custom-call(f32[128,128]{1,0:T(8,128)S(1)} %cholesky.275), custom_call_target="Cholesky" | custom-call | tf_op jit(solution)/shard_map/jit(cholesky)/cholesky | solution.py:66
  236.8 0.7 compare_reduce_fusion.1
  237.6 9.8 %custom-call.29 = f32[1,128,128]{1,2,0:T(8,128)S(1)} custom-call(f32[1,128,128]{2,1,0:T(8,128)S(1)} %get-tuple-element.9), custom_call_target="InvertDiagBlocksLowerTriangular" | custom-call | tf_op jit(solution)/shard_map/jit(cholesky)/cholesky | solution.py:66
  247.6 0.4 convolution_subtract_fusion.2
  248.0 11.7 %cholesky.255 = f32[128,128]{1,0:T(8,128)S(1)} custom-call(f32[128,128]{1,0:T(8,128)S(1)} %convolution_subtract_fusion.2), custom_call_target="Cholesky" | custom-call | tf_op jit(solution)/shard_map/jit(cholesky)/cholesky | solution.py:66
  259.7 0.6 compare_reduce_fusion
  260.4 0.7 compare_reduce_fusion.2
  263.6 1.0 copy.13
  (40 shorter events, 3.7 us)
Async XLA Ops:
  7.2 171.2 %all-reduce.3.cloned.1.call-start = ((), (), s32[]{:S(2)}) async-start(), calls=%async_computation.1 | async-start | bytes 2097152 | tf_op jit(solution)/shard_map/psum | solution.py:65
  13.8 7.1 %copy-start.4 = (s32[1024]{0:T(1024)S(1)}, s32[1024]{0:T(1024)}, u32[]{:S(2)}) copy-start(s32[1024]{0:T(1024)} %param.6) | copy-start | bytes 12292
  13.8 7.1 %copy-start.1 = (f32[1024,256]{1,0:T(8,128)S(1)}, f32[1024,256]{1,0:T(8,128)}, u32[]{:S(2)}) copy-start(f32[1024,256]{1,0:T(8,128)} %param.5) | copy-start | bytes 3145732
  21.1 3.6 %copy-start.3 = (s32[1024]{0:T(1024)S(1)}, s32[1024]{0:T(1024)}, u32[]{:S(2)}) copy-start(s32[1024]{0:T(1024)} %param.7) | copy-start | bytes 12292
  63.3 117.1 %copy-start.2 = (f32[64,256]{1,0:T(8,128)}, f32[64,256]{1,0:T(8,128)S(1)}, u32[]{:S(2)}) copy-start(f32[64,256]{1,0:T(8,128)S(1)} %reduce_sum.9) | copy-start | bytes 196612
  178.3 1.8 copy-start
Sparse Core Ops, SparseCore 0:
  67.6 110.7 all-reduce.2
where the time goes:
time: 272 us; the launch traced here: 271 us
  waiting for transfers between devices  111 us (41%)
  other arithmetic  89.4 us (33%)
  blocking collectives  36.5 us (13%)
  between operations  16.9 us (6%)
  local copies, waits for them, and re-layouts  11 us (4%)
  matrix products  6.7 us (2%)
    psum x1, waiting for transfers between devices, body(): gram = lax.psum(partial_gram, 'rows') / kept_total  111 us
    another operation x14, other arithmetic, body(): factor = jnp.linalg.cholesky(gram).T  78.6 us
    all_to_all x1, blocking collectives, body(): lax.all_to_all(outgoing, 'rows', split_axis=0, concat_axis=0, tiled=True)  34.5 us
    mul x6, other arithmetic, hadamard(): matrix = jnp.kron(matrix, base)  7.1 us
  transfers between devices with their start and end apart: 1, of which 1 were waited for; matrix products, arithmetic and copies ran while one was open for 0% of the time, Pallas kernels for 0%

commit v1 on v0

--- a/solution.py
+++ b/solution.py
@@ -62,7 +62,7 @@
     partial_gram = jnp.dot(
         whole.T, whole, precision=lax.Precision.HIGHEST, preferred_element_type=jnp.float32
     )
-    gram = lax.psum(partial_gram, "rows") / kept_total
+    gram = jnp.sum(lax.all_gather(partial_gram, "rows"), axis=0) / kept_total
     factor = jnp.linalg.cholesky(gram).T
     return (sketch, lax.dynamic_slice_in_dim(factor, column * widths, widths, 1))
 

time: 272 us -> 359 us (1.32)
  waiting for transfers between devices: 111 us -> 190 us
  other arithmetic: 89.4 us -> 97.6 us
    all_gather x0 -> x1, waiting for transfers between devices: none -> 189 us  [body(): gram = jnp.sum(lax.all_gather(partial_gram, 'rows'), axis=0) / kept_total]
    psum x1 -> x0, waiting for transfers between devices: 111 us -> none  [body(): gram = lax.psum(partial_gram, 'rows') / kept_total]
    reduce_sum x0 -> x1, other arithmetic: none -> 7.91 us  [body(): gram = jnp.sum(lax.all_gather(partial_gram, 'rows'), axis=0) / kept_total]
where the time goes in v1:
time: 359 us; the launch traced here: 358 us
  waiting for transfers between devices  190 us (53%)
  other arithmetic  97.6 us (27%)
  blocking collectives  36.5 us (10%)
  between operations  16.8 us (5%)
  local copies, waits for them, and re-layouts  11 us (3%)
  matrix products  6.67 us (2%)
    all_gather x1, waiting for transfers between devices, body(): gram = jnp.sum(lax.all_gather(partial_gram, 'rows'), axis=0) / kept_total  189 us
    another operation x14, other arithmetic, body(): factor = jnp.linalg.cholesky(gram).T  78.9 us
    all_to_all x1, blocking collectives, body(): lax.all_to_all(outgoing, 'rows', split_axis=0, concat_axis=0, tiled=True)  34.5 us
    reduce_sum x1, other arithmetic, body(): gram = jnp.sum(lax.all_gather(partial_gram, 'rows'), axis=0) / kept_total  7.91 us
  transfers between devices with their start and end apart: 1, of which 1 were waited for; matrix products, arithmetic and copies ran while one was open for 0% of the time, Pallas kernels for 0%

profile of v1, /device:TPU:0, one launch (start us, length us, event | category | flops | bytes accessed | tf_op | source)
XLA Modules:
  0.0 358.2 jit_solution(8555973269442215152)
XLA Ops:
  7.2 0.7 compare_and_fusion
  7.9 0.7 broadcast_clamp_fusion
  8.6 0.8 broadcast_multiply_fusion.6
  9.5 0.8 broadcast_multiply_fusion.5
  10.5 0.7 fusion.19
  11.3 0.7 convert_element_type.6
  12.0 0.8 broadcast_multiply_fusion.4
  12.8 0.8 broadcast_multiply_fusion.3
  13.8 0.9 broadcast_multiply_fusion.1
  14.7 0.6 mul.278
  15.3 3.1 broadcast_multiply_fusion
  18.4 4.0 %reshape.203 = f32[128,128,1]{1,0,2:T(8,128)S(1)} reshape(f32[64,2,64,2]{3,2,1,0:T(8,128)} %broadcast_multiply_fusion) | data formatting | bytes 131072 | tf_op jit(solution)/shard_map/jit(kron)/mul | solution.py:12
  22.6 1.8 convolution_bitcast_fusion
  24.5 0.5 copy.13
  24.9 1.0 fusion.21
  26.3 3.5 gather_fusion
  30.1 34.5 %all_to_all.5 = f32[16,64,256]{2,1,0:T(8,128)S(1)} all-to-all(f32[16,64,256]{2,1,0:T(8,128)S(1)} %select_multiply_fusion), channel_id=1, replica_groups=mesh['rows'=16,'cols'=2] {'rows'}, dimensions={0} | all-to-all | bytes 2097152 | tf_op jit(solution)/shard_map/all_to_all | solution.py:58
  64.6 2.1 all_gather.9
  66.7 2.0 fusion.22
  68.7 189.5 %all-gather.3.cloned.1.call-done = f32[8192,512]{1,0:T(8,128)} async-done(((f32[512,512]{1,0:T(8,128)}), f32[8192,512]{1,0:T(8,128)}) %all-gather.3.cloned.1.call-update) | async-done | bytes 16777232 | tf_op jit(solution)/shard_map/all_gather | solution.py:65
  258.2 7.9 %reduce_sum.21 = f32[512,512]{1,0:T(8,128)S(1)} reduce(f32[16,512,512]{2,1,0:T(8,128)} %bitcast.45, f32[]{:T(128)} %constant.195.clone.1), dimensions={0}, to_apply=%region_1.2 | reduce | flops 3932160 | bytes 17825796 | tf_op jit(solution)/shard_map/reduce_sum | solution.py:65
  266.7 11.7 %cholesky.104 = f32[128,128]{1,0:T(8,128)S(1)} custom-call(f32[128,128]{1,0:T(8,128)S(1)} %cholesky.266), custom_call_target="Cholesky" | custom-call | tf_op jit(solution)/shard_map/jit(cholesky)/cholesky | solution.py:66
  278.6 9.8 %custom-call.27 = f32[1,128,128]{1,2,0:T(8,128)S(1)} custom-call(f32[1,128,128]{2,1,0:T(8,128)S(1)} %get-tuple-element.17), custom_call_target="InvertDiagBlocksLowerTriangular" | custom-call | tf_op jit(solution)/shard_map/jit(cholesky)/cholesky | solution.py:66
  289.1 11.9 %cholesky.217 = f32[128,128]{1,0:T(8,128)S(1)} custom-call(f32[128,128]{1,0:T(8,128)S(1)} %cholesky.270), custom_call_target="Cholesky" | custom-call | tf_op jit(solution)/shard_map/jit(cholesky)/cholesky | solution.py:66
  301.1 9.8 %custom-call.28 = f32[1,128,128]{1,2,0:T(8,128)S(1)} custom-call(f32[1,128,128]{2,1,0:T(8,128)S(1)} %get-tuple-element.14), custom_call_target="InvertDiagBlocksLowerTriangular" | custom-call | tf_op jit(solution)/shard_map/jit(cholesky)/cholesky | solution.py:66
  311.6 11.7 %cholesky.238 = f32[128,128]{1,0:T(8,128)S(1)} custom-call(f32[128,128]{1,0:T(8,128)S(1)} %cholesky.275), custom_call_target="Cholesky" | custom-call | tf_op jit(solution)/shard_map/jit(cholesky)/cholesky | solution.py:66
  323.3 0.7 compare_reduce_fusion.1
  324.0 9.8 %custom-call.29 = f32[1,128,128]{1,2,0:T(8,128)S(1)} custom-call(f32[1,128,128]{2,1,0:T(8,128)S(1)} %get-tuple-element.11), custom_call_target="InvertDiagBlocksLowerTriangular" | custom-call | tf_op jit(solution)/shard_map/jit(cholesky)/cholesky | solution.py:66
  334.4 12.0 %cholesky.255 = f32[128,128]{1,0:T(8,128)S(1)} custom-call(f32[128,128]{1,0:T(8,128)S(1)} %convolution_subtract_fusion.2), custom_call_target="Cholesky" | custom-call | tf_op jit(solution)/shard_map/jit(cholesky)/cholesky | solution.py:66
  346.4 0.6 compare_reduce_fusion
  347.1 0.7 compare_reduce_fusion.2
  350.4 1.0 copy.16
  (34 shorter events, 4.4 us)
Async XLA Ops:
  7.2 251.1 %all-gather.3.cloned.1.call-start = ((), (), s32[]{:S(2)}) async-start(), calls=%async_computation.1 | async-start | bytes 17825792 | tf_op jit(solution)/shard_map/all_gather | solution.py:65
  15.3 7.1 %copy-start = (f32[1024,256]{1,0:T(8,128)S(1)}, f32[1024,256]{1,0:T(8,128)}, u32[]{:S(2)}) copy-start(f32[1024,256]{1,0:T(8,128)} %param.5) | copy-start | bytes 3145732
  64.6 201.5 %copy-start.1 = (f32[64,256]{1,0:T(8,128)}, f32[64,256]{1,0:T(8,128)S(1)}, u32[]{:S(2)}) copy-start(f32[64,256]{1,0:T(8,128)S(1)} %reduce_sum.20) | copy-start | bytes 196612
Sparse Core Ops, SparseCore 0:
  68.9 189.3 all-gather.2
